TPU v7x, 64 devices: a 2x2x8 block of a 4x4x8 slice. The times are simulated.
64 devices in a mesh: dp: 4 (over x, y), seq: 16 (over z, core).
Axes of the slice: x: 2, y: 2, z: 8, core: 2. Of those that a mesh axis runs over, the one named last changes fastest.
The devices are a block of a 4x4x8 slice.
Arguments:
- enc_out: bfloat16 [64, 384, 1024], P('dp', 'seq'), parts along dimension 0
- pred_out: bfloat16 [64, 24, 320], P('dp'), parts along dimension 0
- w_enc: bfloat16 [1024, 512], replicated
- w_pred: bfloat16 [320, 512], replicated
- w_out: bfloat16 [512, 1024], replicated
- b_out: float32 [1024], replicated
- labels: int32 [64, 23], P('dp'), parts along dimension 0
- frame_len: int32 [64], P('dp'), parts along dimension 0
- label_len: int32 [64], P('dp'), parts along dimension 0
Outputs:
- output: float32 [64], P('dp'), parts along dimension 0
There are 4 independent parts. A program takes and returns all parts, laid end to end along the dimension named above; an argument that names none is the same for every part.
All inputs are finite; a program needn't handle non-finite values.
Results may differ from a plain program's by a relative error of at most 0.001.
Values are sent between devices in bfloat16 or wider.
A program may use at most 768 MiB of HBM per device.

v0:
```python
import functools
import jax
import jax.numpy as jnp
from jax import lax
from jax.sharding import PartitionSpec as P

NEG_FILL = -1.0e30


def frame_logprobs(enc_rows, pred_f32, w_out, b_out, w_label, b_label):
    hidden = jnp.tanh(enc_rows.astype(jnp.float32)[:, :, None, :] + pred_f32[None]).astype(jnp.bfloat16)
    logits = jnp.einsum("kbpj,jv->kbpv", hidden, w_out, preferred_element_type=jnp.float32) + b_out
    log_norm = jax.nn.logsumexp(logits, axis=-1)
    blank_lp = logits[..., 0] - log_norm
    label_dot = jnp.einsum("kbpj,jbp->kbp", hidden[:, :, :-1, :], w_label, preferred_element_type=jnp.float32)
    label_lp = label_dot + b_label - log_norm[:, :, :-1]
    return blank_lp, label_lp


def alpha_rows(row_in, blank_all, cum_all):
    def frame_step(row_prev, step_in):
        blank_lp, cum_label = step_in
        row_next = cum_label + lax.cumlogsumexp(row_prev - cum_label, axis=1) + blank_lp
        return row_next, row_next
    return lax.scan(frame_step, row_in, (blank_all, cum_all))


def solution(mesh):
    n_seq = mesh.shape["seq"]
    shift_perm = [(src, src + 1) for src in range(n_seq - 1)]

    def local_loss(enc_blk, pred_out, w_enc, w_pred, w_out, b_out, labels, frame_len, label_len):
        n_utt = enc_blk.shape[0]
        t_local = enc_blk.shape[1]
        n_pos = pred_out.shape[1]
        seq_idx = lax.axis_index("seq")
        enc_proj = jnp.einsum("bth,hj->tbj", enc_blk, w_enc, preferred_element_type=jnp.float32).astype(jnp.bfloat16)
        pred_f32 = jnp.einsum("bph,hj->bpj", pred_out, w_pred, preferred_element_type=jnp.float32).astype(jnp.bfloat16).astype(jnp.float32)
        step_fn = functools.partial(frame_logprobs, pred_f32=pred_f32, w_out=w_out, b_out=b_out, w_label=jnp.take(w_out, labels, axis=1), b_label=jnp.take(b_out, labels))
        blank_all, label_all = lax.map(step_fn, enc_proj[:, None])
        blank_all = blank_all[:, 0]
        cum_all = jnp.concatenate([jnp.zeros((t_local, n_utt, 1), jnp.float32), jnp.cumsum(label_all[:, 0], axis=2)], axis=2)
        positions = jnp.arange(n_pos)
        start_row = jnp.broadcast_to(jnp.where(positions == 0, 0.0, NEG_FILL), (n_utt, n_pos)).astype(jnp.float32)

        def relay_hop(hop_idx, row_in):
            last_row, _ = alpha_rows(row_in, blank_all, cum_all)
            passed = lax.ppermute(last_row, "seq", shift_perm)
            return jnp.where(seq_idx == 0, start_row, passed)

        entry_row = lax.fori_loop(0, n_seq - 1, relay_hop, start_row)
        _, alpha_all = alpha_rows(entry_row, blank_all, cum_all)
        frame_ids = seq_idx * t_local + jnp.arange(t_local)
        end_frame = frame_ids[:, None] == frame_len[None, :] - 1
        end_pos = positions[None, :] == label_len[:, None]
        picked = jnp.sum(jnp.where(end_frame[:, :, None] & end_pos[None], alpha_all, 0.0), axis=(0, 2))
        return -lax.psum(picked, "seq")

    in_specs = (P("dp", "seq", None), P("dp", None, None), P(), P(), P(), P(), P("dp", None), P("dp"), P("dp"))
    return jax.shard_map(local_loss, mesh=mesh, in_specs=in_specs, out_specs=P("dp"), check_vma=False)
```

profile of v0, /device:TPU:21, one launch (start us, length us, event | category | flops | bytes accessed | tf_op | source)
XLA Modules:
  0.0 463.4 jit_solution(13937372547409106633)
XLA Ops:
  0.0 1.2 copy-done
  1.2 1.8 fusion.19
  3.0 0.9 copy.15
  4.2 1.5 copy.14
  5.9 2.1 gather_fusion
  8.0 0.9 reshape.185
  8.8 1.9 gather_fusion.1
  11.1 0.8 copy-done.2
  11.9 80.3 %while.59 = (s32[]{:T(128)}, f32[24,1,16,24]{3,2,1,0:T(8,128)S(1)}, f32[24,1,16,23]{3,2,1,0:T(8,128)}, bf16[24,1,16,512]{3,2,1,0:T(8,128)(2,1)}, f32[16,24,512]{...) while((s32[]{:T(128)}, f32[24,1,16,24]{3,2,1,0:T(8,128)S(1)}, ...), condition=%wide.region_3.4_spmd.clone, body=%wide.region_0.3_spmd.sunk.clone | while | flops 405761728 | bytes 7802545 | solution.py:40
  92.2 10.6 %reduce_window_sum.11 = f32[24,16,23]{2,1,0:T(8,128)S(1)} reduce-window(f32[24,16,23]{2,1,0:T(8,128)} %bitcast.128, f32[]{:T(128)} %constant.98.clone.1), window={size=1x1x23 pad=0_0x0_0x22_0}, to_apply=%region_4.5 | reduce-window | flops 194304 | bytes 70660 | tf_op jit(solution)/shard_map/jit(cumsum)/reduce_window_sum | solution.py:42
  103.0 310.0 %while.62 = (s32[]{:T(128)}, f32[16,24]{1,0:T(8,128)S(1)}, pred[]{:T(512)}, f32[24,16,24]{2,1,0:T(8,128)S(1)}, f32[24,16,24]{2,1,0:T(8,128)S(1)}, /*index=5*/f32[24]{0:T(128)S(1)}, s32[]{:T(128)}, s32[]{:T(128)}, f32[]{:T(128)}) while((s32[]{:T(128)}, f32[16,24]{1,0:T(8,128)S(1)}, pred[]{:T(512)}, ...), condition=%wide.region_9.10_spmd.clone.clone, body=%wide.region_5.9_spmd.clone.sunk.clone | while | flops 72196 | bytes 23415 | solution.py:51
  103.0 15.3 %while.61 = (s32[]{:T(128)}, f32[16,24]{1,0:T(8,128)S(1)}, f32[24,16,24]{2,1,0:T(8,128)S(1)}, f32[24,16,24]{2,1,0:T(8,128)S(1)}, s32[]{:T(128)}, /*index=5*/f32[]{:T(128)}) while((s32[]{:T(128)}, f32[16,24]{1,0:T(8,128)S(1)}, f32[24,16,24]{2,1,0:T(8,128)S(1)}, f32[24,16,24]{2,1,0:T(8,128)S(1)}, s32[]{:T(128)}, /*index=5*/f32[]{:T(128)}) %tuple.88), condition=%wide.region_8.8_spmd, body=%wide.region_6.7_spmd.sunk | while | flops 71810 | bytes 13913 | solution.py:25
  118.4 5.1 %collective-permute-start = (f32[16,24]{1,0:T(8,128)S(1)}, f32[16,24]{1,0:T(8,128)S(1)}, u32[]{:S(2)}, u32[]{:S(2)}) collective-permute-start(f32[16,24]{1,0:T(8,128)S(1)} %get-tuple-element.470), channel_id=1, source_target_pairs={{0,1},{1,2},{2,3},{3,4},{4,5},{5,6},{6,7},{7,8},{8,9},{9,10},{10,1... | collective-permute-start | bytes 4616 | tf_op jit(solution)/shard_map/while/body/eval_jaxpr/ppermute | solution.py:48
  123.5 1.5 collective-permute-done
  125.0 15.3 %while.61 = (s32[]{:T(128)}, f32[16,24]{1,0:T(8,128)S(1)}, f32[24,16,24]{2,1,0:T(8,128)S(1)}, f32[24,16,24]{2,1,0:T(8,128)S(1)}, s32[]{:T(128)}, /*index=5*/f32[]{:T(128)}) while((s32[]{:T(128)}, f32[16,24]{1,0:T(8,128)S(1)}, f32[24,16,24]{2,1,0:T(8,128)S(1)}, f32[24,16,24]{2,1,0:T(8,128)S(1)}, s32[]{:T(128)}, /*index=5*/f32[]{:T(128)}) %tuple.88), condition=%wide.region_8.8_spmd, body=%wide.region_6.7_spmd.sunk | while | flops 71810 | bytes 13913 | solution.py:25
  140.3 3.5 collective-permute-start
  143.8 0.8 collective-permute-done
  144.6 15.3 %while.61 = (s32[]{:T(128)}, f32[16,24]{1,0:T(8,128)S(1)}, f32[24,16,24]{2,1,0:T(8,128)S(1)}, f32[24,16,24]{2,1,0:T(8,128)S(1)}, s32[]{:T(128)}, /*index=5*/f32[]{:T(128)}) while((s32[]{:T(128)}, f32[16,24]{1,0:T(8,128)S(1)}, f32[24,16,24]{2,1,0:T(8,128)S(1)}, f32[24,16,24]{2,1,0:T(8,128)S(1)}, s32[]{:T(128)}, /*index=5*/f32[]{:T(128)}) %tuple.88), condition=%wide.region_8.8_spmd, body=%wide.region_6.7_spmd.sunk | while | flops 71810 | bytes 13913 | solution.py:25
  159.9 4.2 collective-permute-start
  164.2 0.8 collective-permute-done
  164.9 15.3 %while.61 = (s32[]{:T(128)}, f32[16,24]{1,0:T(8,128)S(1)}, f32[24,16,24]{2,1,0:T(8,128)S(1)}, f32[24,16,24]{2,1,0:T(8,128)S(1)}, s32[]{:T(128)}, /*index=5*/f32[]{:T(128)}) while((s32[]{:T(128)}, f32[16,24]{1,0:T(8,128)S(1)}, f32[24,16,24]{2,1,0:T(8,128)S(1)}, f32[24,16,24]{2,1,0:T(8,128)S(1)}, s32[]{:T(128)}, /*index=5*/f32[]{:T(128)}) %tuple.88), condition=%wide.region_8.8_spmd, body=%wide.region_6.7_spmd.sunk | while | flops 71810 | bytes 13913 | solution.py:25
  180.3 4.2 collective-permute-start
  184.5 0.8 collective-permute-done
  185.3 15.3 %while.61 = (s32[]{:T(128)}, f32[16,24]{1,0:T(8,128)S(1)}, f32[24,16,24]{2,1,0:T(8,128)S(1)}, f32[24,16,24]{2,1,0:T(8,128)S(1)}, s32[]{:T(128)}, /*index=5*/f32[]{:T(128)}) while((s32[]{:T(128)}, f32[16,24]{1,0:T(8,128)S(1)}, f32[24,16,24]{2,1,0:T(8,128)S(1)}, f32[24,16,24]{2,1,0:T(8,128)S(1)}, s32[]{:T(128)}, /*index=5*/f32[]{:T(128)}) %tuple.88), condition=%wide.region_8.8_spmd, body=%wide.region_6.7_spmd.sunk | while | flops 71810 | bytes 13913 | solution.py:25
  200.6 4.2 collective-permute-start
  204.8 0.8 collective-permute-done
  205.6 15.3 %while.61 = (s32[]{:T(128)}, f32[16,24]{1,0:T(8,128)S(1)}, f32[24,16,24]{2,1,0:T(8,128)S(1)}, f32[24,16,24]{2,1,0:T(8,128)S(1)}, s32[]{:T(128)}, /*index=5*/f32[]{:T(128)}) while((s32[]{:T(128)}, f32[16,24]{1,0:T(8,128)S(1)}, f32[24,16,24]{2,1,0:T(8,128)S(1)}, f32[24,16,24]{2,1,0:T(8,128)S(1)}, s32[]{:T(128)}, /*index=5*/f32[]{:T(128)}) %tuple.88), condition=%wide.region_8.8_spmd, body=%wide.region_6.7_spmd.sunk | while | flops 71810 | bytes 13913 | solution.py:25
  220.9 4.2 collective-permute-start
  226.0 15.3 %while.61 = (s32[]{:T(128)}, f32[16,24]{1,0:T(8,128)S(1)}, f32[24,16,24]{2,1,0:T(8,128)S(1)}, f32[24,16,24]{2,1,0:T(8,128)S(1)}, s32[]{:T(128)}, /*index=5*/f32[]{:T(128)}) while((s32[]{:T(128)}, f32[16,24]{1,0:T(8,128)S(1)}, f32[24,16,24]{2,1,0:T(8,128)S(1)}, f32[24,16,24]{2,1,0:T(8,128)S(1)}, s32[]{:T(128)}, /*index=5*/f32[]{:T(128)}) %tuple.88), condition=%wide.region_8.8_spmd, body=%wide.region_6.7_spmd.sunk | while | flops 71810 | bytes 13913 | solution.py:25
  241.3 4.2 collective-permute-start
  246.3 15.3 %while.61 = (s32[]{:T(128)}, f32[16,24]{1,0:T(8,128)S(1)}, f32[24,16,24]{2,1,0:T(8,128)S(1)}, f32[24,16,24]{2,1,0:T(8,128)S(1)}, s32[]{:T(128)}, /*index=5*/f32[]{:T(128)}) while((s32[]{:T(128)}, f32[16,24]{1,0:T(8,128)S(1)}, f32[24,16,24]{2,1,0:T(8,128)S(1)}, f32[24,16,24]{2,1,0:T(8,128)S(1)}, s32[]{:T(128)}, /*index=5*/f32[]{:T(128)}) %tuple.88), condition=%wide.region_8.8_spmd, body=%wide.region_6.7_spmd.sunk | while | flops 71810 | bytes 13913 | solution.py:25
  261.6 4.2 collective-permute-start
  266.6 15.3 %while.61 = (s32[]{:T(128)}, f32[16,24]{1,0:T(8,128)S(1)}, f32[24,16,24]{2,1,0:T(8,128)S(1)}, f32[24,16,24]{2,1,0:T(8,128)S(1)}, s32[]{:T(128)}, /*index=5*/f32[]{:T(128)}) while((s32[]{:T(128)}, f32[16,24]{1,0:T(8,128)S(1)}, f32[24,16,24]{2,1,0:T(8,128)S(1)}, f32[24,16,24]{2,1,0:T(8,128)S(1)}, s32[]{:T(128)}, /*index=5*/f32[]{:T(128)}) %tuple.88), condition=%wide.region_8.8_spmd, body=%wide.region_6.7_spmd.sunk | while | flops 71810 | bytes 13913 | solution.py:25
  282.0 4.2 collective-permute-start
  287.0 15.3 %while.61 = (s32[]{:T(128)}, f32[16,24]{1,0:T(8,128)S(1)}, f32[24,16,24]{2,1,0:T(8,128)S(1)}, f32[24,16,24]{2,1,0:T(8,128)S(1)}, s32[]{:T(128)}, /*index=5*/f32[]{:T(128)}) while((s32[]{:T(128)}, f32[16,24]{1,0:T(8,128)S(1)}, f32[24,16,24]{2,1,0:T(8,128)S(1)}, f32[24,16,24]{2,1,0:T(8,128)S(1)}, s32[]{:T(128)}, /*index=5*/f32[]{:T(128)}) %tuple.88), condition=%wide.region_8.8_spmd, body=%wide.region_6.7_spmd.sunk | while | flops 71810 | bytes 13913 | solution.py:25
  302.3 4.2 collective-permute-start
  307.3 15.3 %while.61 = (s32[]{:T(128)}, f32[16,24]{1,0:T(8,128)S(1)}, f32[24,16,24]{2,1,0:T(8,128)S(1)}, f32[24,16,24]{2,1,0:T(8,128)S(1)}, s32[]{:T(128)}, /*index=5*/f32[]{:T(128)}) while((s32[]{:T(128)}, f32[16,24]{1,0:T(8,128)S(1)}, f32[24,16,24]{2,1,0:T(8,128)S(1)}, f32[24,16,24]{2,1,0:T(8,128)S(1)}, s32[]{:T(128)}, /*index=5*/f32[]{:T(128)}) %tuple.88), condition=%wide.region_8.8_spmd, body=%wide.region_6.7_spmd.sunk | while | flops 71810 | bytes 13913 | solution.py:25
  322.6 4.2 collective-permute-start
  327.7 15.3 %while.61 = (s32[]{:T(128)}, f32[16,24]{1,0:T(8,128)S(1)}, f32[24,16,24]{2,1,0:T(8,128)S(1)}, f32[24,16,24]{2,1,0:T(8,128)S(1)}, s32[]{:T(128)}, /*index=5*/f32[]{:T(128)}) while((s32[]{:T(128)}, f32[16,24]{1,0:T(8,128)S(1)}, f32[24,16,24]{2,1,0:T(8,128)S(1)}, f32[24,16,24]{2,1,0:T(8,128)S(1)}, s32[]{:T(128)}, /*index=5*/f32[]{:T(128)}) %tuple.88), condition=%wide.region_8.8_spmd, body=%wide.region_6.7_spmd.sunk | while | flops 71810 | bytes 13913 | solution.py:25
  343.0 4.6 collective-permute-start
  348.4 15.3 %while.61 = (s32[]{:T(128)}, f32[16,24]{1,0:T(8,128)S(1)}, f32[24,16,24]{2,1,0:T(8,128)S(1)}, f32[24,16,24]{2,1,0:T(8,128)S(1)}, s32[]{:T(128)}, /*index=5*/f32[]{:T(128)}) while((s32[]{:T(128)}, f32[16,24]{1,0:T(8,128)S(1)}, f32[24,16,24]{2,1,0:T(8,128)S(1)}, f32[24,16,24]{2,1,0:T(8,128)S(1)}, s32[]{:T(128)}, /*index=5*/f32[]{:T(128)}) %tuple.88), condition=%wide.region_8.8_spmd, body=%wide.region_6.7_spmd.sunk | while | flops 71810 | bytes 13913 | solution.py:25
  363.7 5.4 %collective-permute-start = (f32[16,24]{1,0:T(8,128)S(1)}, f32[16,24]{1,0:T(8,128)S(1)}, u32[]{:S(2)}, u32[]{:S(2)}) collective-permute-start(f32[16,24]{1,0:T(8,128)S(1)} %get-tuple-element.470), channel_id=1, source_target_pairs={{0,1},{1,2},{2,3},{3,4},{4,5},{5,6},{6,7},{7,8},{8,9},{9,10},{10,1... | collective-permute-start | bytes 4616 | tf_op jit(solution)/shard_map/while/body/eval_jaxpr/ppermute | solution.py:48
  369.9 15.3 %while.61 = (s32[]{:T(128)}, f32[16,24]{1,0:T(8,128)S(1)}, f32[24,16,24]{2,1,0:T(8,128)S(1)}, f32[24,16,24]{2,1,0:T(8,128)S(1)}, s32[]{:T(128)}, /*index=5*/f32[]{:T(128)}) while((s32[]{:T(128)}, f32[16,24]{1,0:T(8,128)S(1)}, f32[24,16,24]{2,1,0:T(8,128)S(1)}, f32[24,16,24]{2,1,0:T(8,128)S(1)}, s32[]{:T(128)}, /*index=5*/f32[]{:T(128)}) %tuple.88), condition=%wide.region_8.8_spmd, body=%wide.region_6.7_spmd.sunk | while | flops 71810 | bytes 13913 | solution.py:25
  385.3 5.4 %collective-permute-start = (f32[16,24]{1,0:T(8,128)S(1)}, f32[16,24]{1,0:T(8,128)S(1)}, u32[]{:S(2)}, u32[]{:S(2)}) collective-permute-start(f32[16,24]{1,0:T(8,128)S(1)} %get-tuple-element.470), channel_id=1, source_target_pairs={{0,1},{1,2},{2,3},{3,4},{4,5},{5,6},{6,7},{7,8},{8,9},{9,10},{10,1... | collective-permute-start | bytes 4616 | tf_op jit(solution)/shard_map/while/body/eval_jaxpr/ppermute | solution.py:48
  391.5 15.3 %while.61 = (s32[]{:T(128)}, f32[16,24]{1,0:T(8,128)S(1)}, f32[24,16,24]{2,1,0:T(8,128)S(1)}, f32[24,16,24]{2,1,0:T(8,128)S(1)}, s32[]{:T(128)}, /*index=5*/f32[]{:T(128)}) while((s32[]{:T(128)}, f32[16,24]{1,0:T(8,128)S(1)}, f32[24,16,24]{2,1,0:T(8,128)S(1)}, f32[24,16,24]{2,1,0:T(8,128)S(1)}, s32[]{:T(128)}, /*index=5*/f32[]{:T(128)}) %tuple.88), condition=%wide.region_8.8_spmd, body=%wide.region_6.7_spmd.sunk | while | flops 71810 | bytes 13913 | solution.py:25
  406.8 5.4 %collective-permute-start = (f32[16,24]{1,0:T(8,128)S(1)}, f32[16,24]{1,0:T(8,128)S(1)}, u32[]{:S(2)}, u32[]{:S(2)}) collective-permute-start(f32[16,24]{1,0:T(8,128)S(1)} %get-tuple-element.470), channel_id=1, source_target_pairs={{0,1},{1,2},{2,3},{3,4},{4,5},{5,6},{6,7},{7,8},{8,9},{9,10},{10,1... | collective-permute-start | bytes 4616 | tf_op jit(solution)/shard_map/while/body/eval_jaxpr/ppermute | solution.py:48
  413.0 15.4 %while.60 = (s32[]{:T(128)}, f32[16,24]{1,0:T(8,128)S(1)}, f32[24,16,24]{2,1,0:T(8,128)S(1)}, f32[24,16,24]{2,1,0:T(8,128)S(1)}, f32[24,16,24]{2,1,0:T(8,128)S(1)}) while((s32[]{:T(128)}, f32[16,24]{1,0:T(8,128)S(1)}, f32[24,16,24]{2,1,0:T(8,128)S(1)}, f32[24,16,24]{2,1,0:T(8,128)S(1)}, f32[24,16,24]{2,1,0:T(8,128)S(1)}) %tuple.104), condition=%wide.region_12.13_spmd.clone, body=%wide.region_10.12_spmd.sunk.clone | while | flops 72578 | bytes 46677 | solution.py:25
  428.8 34.1 %psum.7 = f32[16]{0:T(128)S(1)} all-reduce(f32[16]{0:T(128)S(1)} %select_reduce_fusion), channel_id=1, replica_groups=mesh['dp'=4,'seq'=16] {'seq'}, use_global_device_ids=true, to_apply=%region_14.15 | all-reduce | flops 16 | bytes 128 | tf_op jit(solution)/shard_map/psum | solution.py:57
  (1501 shorter events, 333.0 us)
Async XLA Ops:
  0.0 1.2 copy-start
  1.2 2.6 copy-start.4
  1.2 2.6 copy-start.5
  3.9 1.9 copy-start.6
  7.9 0.9 copy-start.1
  8.8 2.0 copy-start.3
  10.7 1.2 copy-start.2
  103.0 325.5 %copy-start.7 = (s32[16]{0:T(128)S(1)}, s32[16]{0:T(128)}, u32[]{:S(2)}) copy-start(s32[16]{0:T(128)} %param.25) | copy-start | bytes 196
  103.0 325.5 %copy-start.8 = (s32[16]{0:T(128)S(1)}, s32[16]{0:T(128)}, u32[]{:S(2)}) copy-start(s32[16]{0:T(128)} %param.24) | copy-start | bytes 196
  118.4 6.6 %collective-permute-start = (f32[16,24]{1,0:T(8,128)S(1)}, f32[16,24]{1,0:T(8,128)S(1)}, u32[]{:S(2)}, u32[]{:S(2)}) collective-permute-start(f32[16,24]{1,0:T(8,128)S(1)} %get-tuple-element.470), channel_id=1, source_target_pairs={{0,1},{1,2},{2,3},{3,4},{4,5},{5,6},{6,7},{7,8},{8,9},{9,10},{10,1... | collective-permute-start | bytes 4616 | tf_op jit(solution)/shard_map/while/body/eval_jaxpr/ppermute | solution.py:48
  140.3 4.3 collective-permute-start
  159.9 5.0 %collective-permute-start = (f32[16,24]{1,0:T(8,128)S(1)}, f32[16,24]{1,0:T(8,128)S(1)}, u32[]{:S(2)}, u32[]{:S(2)}) collective-permute-start(f32[16,24]{1,0:T(8,128)S(1)} %get-tuple-element.470), channel_id=1, source_target_pairs={{0,1},{1,2},{2,3},{3,4},{4,5},{5,6},{6,7},{7,8},{8,9},{9,10},{10,1... | collective-permute-start | bytes 4616 | tf_op jit(solution)/shard_map/while/body/eval_jaxpr/ppermute | solution.py:48
  180.3 5.0 %collective-permute-start = (f32[16,24]{1,0:T(8,128)S(1)}, f32[16,24]{1,0:T(8,128)S(1)}, u32[]{:S(2)}, u32[]{:S(2)}) collective-permute-start(f32[16,24]{1,0:T(8,128)S(1)} %get-tuple-element.470), channel_id=1, source_target_pairs={{0,1},{1,2},{2,3},{3,4},{4,5},{5,6},{6,7},{7,8},{8,9},{9,10},{10,1... | collective-permute-start | bytes 4616 | tf_op jit(solution)/shard_map/while/body/eval_jaxpr/ppermute | solution.py:48
  200.6 5.0 %collective-permute-start = (f32[16,24]{1,0:T(8,128)S(1)}, f32[16,24]{1,0:T(8,128)S(1)}, u32[]{:S(2)}, u32[]{:S(2)}) collective-permute-start(f32[16,24]{1,0:T(8,128)S(1)} %get-tuple-element.470), channel_id=1, source_target_pairs={{0,1},{1,2},{2,3},{3,4},{4,5},{5,6},{6,7},{7,8},{8,9},{9,10},{10,1... | collective-permute-start | bytes 4616 | tf_op jit(solution)/shard_map/while/body/eval_jaxpr/ppermute | solution.py:48
  220.9 5.0 %collective-permute-start = (f32[16,24]{1,0:T(8,128)S(1)}, f32[16,24]{1,0:T(8,128)S(1)}, u32[]{:S(2)}, u32[]{:S(2)}) collective-permute-start(f32[16,24]{1,0:T(8,128)S(1)} %get-tuple-element.470), channel_id=1, source_target_pairs={{0,1},{1,2},{2,3},{3,4},{4,5},{5,6},{6,7},{7,8},{8,9},{9,10},{10,1... | collective-permute-start | bytes 4616 | tf_op jit(solution)/shard_map/while/body/eval_jaxpr/ppermute | solution.py:48
  241.3 5.0 %collective-permute-start = (f32[16,24]{1,0:T(8,128)S(1)}, f32[16,24]{1,0:T(8,128)S(1)}, u32[]{:S(2)}, u32[]{:S(2)}) collective-permute-start(f32[16,24]{1,0:T(8,128)S(1)} %get-tuple-element.470), channel_id=1, source_target_pairs={{0,1},{1,2},{2,3},{3,4},{4,5},{5,6},{6,7},{7,8},{8,9},{9,10},{10,1... | collective-permute-start | bytes 4616 | tf_op jit(solution)/shard_map/while/body/eval_jaxpr/ppermute | solution.py:48
  261.6 5.0 %collective-permute-start = (f32[16,24]{1,0:T(8,128)S(1)}, f32[16,24]{1,0:T(8,128)S(1)}, u32[]{:S(2)}, u32[]{:S(2)}) collective-permute-start(f32[16,24]{1,0:T(8,128)S(1)} %get-tuple-element.470), channel_id=1, source_target_pairs={{0,1},{1,2},{2,3},{3,4},{4,5},{5,6},{6,7},{7,8},{8,9},{9,10},{10,1... | collective-permute-start | bytes 4616 | tf_op jit(solution)/shard_map/while/body/eval_jaxpr/ppermute | solution.py:48
  282.0 5.0 %collective-permute-start = (f32[16,24]{1,0:T(8,128)S(1)}, f32[16,24]{1,0:T(8,128)S(1)}, u32[]{:S(2)}, u32[]{:S(2)}) collective-permute-start(f32[16,24]{1,0:T(8,128)S(1)} %get-tuple-element.470), channel_id=1, source_target_pairs={{0,1},{1,2},{2,3},{3,4},{4,5},{5,6},{6,7},{7,8},{8,9},{9,10},{10,1... | collective-permute-start | bytes 4616 | tf_op jit(solution)/shard_map/while/body/eval_jaxpr/ppermute | solution.py:48
  302.3 5.0 %collective-permute-start = (f32[16,24]{1,0:T(8,128)S(1)}, f32[16,24]{1,0:T(8,128)S(1)}, u32[]{:S(2)}, u32[]{:S(2)}) collective-permute-start(f32[16,24]{1,0:T(8,128)S(1)} %get-tuple-element.470), channel_id=1, source_target_pairs={{0,1},{1,2},{2,3},{3,4},{4,5},{5,6},{6,7},{7,8},{8,9},{9,10},{10,1... | collective-permute-start | bytes 4616 | tf_op jit(solution)/shard_map/while/body/eval_jaxpr/ppermute | solution.py:48
  322.6 5.0 %collective-permute-start = (f32[16,24]{1,0:T(8,128)S(1)}, f32[16,24]{1,0:T(8,128)S(1)}, u32[]{:S(2)}, u32[]{:S(2)}) collective-permute-start(f32[16,24]{1,0:T(8,128)S(1)} %get-tuple-element.470), channel_id=1, source_target_pairs={{0,1},{1,2},{2,3},{3,4},{4,5},{5,6},{6,7},{7,8},{8,9},{9,10},{10,1... | collective-permute-start | bytes 4616 | tf_op jit(solution)/shard_map/while/body/eval_jaxpr/ppermute | solution.py:48
  343.0 5.4 %collective-permute-start = (f32[16,24]{1,0:T(8,128)S(1)}, f32[16,24]{1,0:T(8,128)S(1)}, u32[]{:S(2)}, u32[]{:S(2)}) collective-permute-start(f32[16,24]{1,0:T(8,128)S(1)} %get-tuple-element.470), channel_id=1, source_target_pairs={{0,1},{1,2},{2,3},{3,4},{4,5},{5,6},{6,7},{7,8},{8,9},{9,10},{10,1... | collective-permute-start | bytes 4616 | tf_op jit(solution)/shard_map/while/body/eval_jaxpr/ppermute | solution.py:48
  363.7 6.2 %collective-permute-start = (f32[16,24]{1,0:T(8,128)S(1)}, f32[16,24]{1,0:T(8,128)S(1)}, u32[]{:S(2)}, u32[]{:S(2)}) collective-permute-start(f32[16,24]{1,0:T(8,128)S(1)} %get-tuple-element.470), channel_id=1, source_target_pairs={{0,1},{1,2},{2,3},{3,4},{4,5},{5,6},{6,7},{7,8},{8,9},{9,10},{10,1... | collective-permute-start | bytes 4616 | tf_op jit(solution)/shard_map/while/body/eval_jaxpr/ppermute | solution.py:48
  385.3 6.2 %collective-permute-start = (f32[16,24]{1,0:T(8,128)S(1)}, f32[16,24]{1,0:T(8,128)S(1)}, u32[]{:S(2)}, u32[]{:S(2)}) collective-permute-start(f32[16,24]{1,0:T(8,128)S(1)} %get-tuple-element.470), channel_id=1, source_target_pairs={{0,1},{1,2},{2,3},{3,4},{4,5},{5,6},{6,7},{7,8},{8,9},{9,10},{10,1... | collective-permute-start | bytes 4616 | tf_op jit(solution)/shard_map/while/body/eval_jaxpr/ppermute | solution.py:48
  406.8 6.2 %collective-permute-start = (f32[16,24]{1,0:T(8,128)S(1)}, f32[16,24]{1,0:T(8,128)S(1)}, u32[]{:S(2)}, u32[]{:S(2)}) collective-permute-start(f32[16,24]{1,0:T(8,128)S(1)} %get-tuple-element.470), channel_id=1, source_target_pairs={{0,1},{1,2},{2,3},{3,4},{4,5},{5,6},{6,7},{7,8},{8,9},{9,10},{10,1... | collective-permute-start | bytes 4616 | tf_op jit(solution)/shard_map/while/body/eval_jaxpr/ppermute | solution.py:48
where the time goes:
time: 469 us; the launch traced here: 463 us
  other arithmetic  314 us (67%)
  starting transfers between devices  67.6 us (14%)
  blocking collectives  34.1 us (7%)
  matrix products  18.3 us (4%)
  local copies, waits for them, and re-layouts  14.8 us (3%)
  waiting for transfers between devices  12.3 us (3%)
    another operation x384, other arithmetic, frame_step(): lax.cumlogsumexp(row_prev - cum_label, axis=1)  238 us
    ppermute x15, starting transfers between devices, relay_hop(): passed = lax.ppermute(last_row, 'seq', shift_perm)  67.6 us
    psum x1, blocking collectives, local_loss(): return -lax.psum(picked, 'seq')  34.1 us
    convert_element_type x24, other arithmetic, frame_logprobs(): enc_rows.astype(jnp.float32)[:, :, None, :] + pred_f32[None]  17.3 us
    dot_general x24, matrix products, frame_logprobs(): jnp.einsum('kbpj,jv->kbpv', hidden, w_out, preferred_element_type=jnp.flo...  16.2 us
    while x48, other arithmetic  15.6 us
    dynamic_update_slice x48, other arithmetic, local_loss(): blank_all, label_all = lax.map(step_fn, enc_proj[:, None])  15.4 us
    ppermute x15, waiting for transfers between devices, relay_hop(): passed = lax.ppermute(last_row, 'seq', shift_perm)  12.3 us
  transfers between devices with their start and end apart: 15, of which 15 were waited for; matrix products, arithmetic and copies ran while one was open for 0% of the time, Pallas kernels for 0%

commit v1 on v0

v1 whole, which is shorter than its diff:
```python
import functools
import jax
import jax.numpy as jnp
from jax import lax
from jax.experimental import pallas as pl
from jax.experimental.pallas import tpu as pltpu
from jax.sharding import PartitionSpec as P

NEG_FILL = -1.0e30
OCT = 8
ITEMS = 32
GROUP = 32
N_HANDLERS = 4
MESH = pl.DeviceIdType.MESH


def joint_kernel(enc_hbm, pred_hbm, wenc_hbm, wpred_hbm, wout_hbm, bout_ref, lab_ref, flen_ref, llen_ref,
                 blank_out, label_out,
                 enc_v, pred_v, wenc_v, wpred_v, wout_v, w_t, bias_t, a_v, c_v, hid, z_a, z_b, mx_v, o_v,
                 lab_pad, tab_v, tab_s, sems, tab_sem):
    n_utt, n_lab = lab_ref.shape
    n_pos = n_lab + 1
    t_local = enc_v.shape[0] // n_utt
    n_oct = t_local // OCT
    joint, vocab = wout_v.shape
    n_rows = n_utt * GROUP
    t0 = lax.axis_index("seq") * t_local

    copies = [
        pltpu.make_async_copy(src, dst, sems.at[k])
        for k, (src, dst) in enumerate([
            (wout_hbm, wout_v), (enc_hbm, enc_v), (wenc_hbm, wenc_v), (pred_hbm, pred_v), (wpred_hbm, wpred_v)])
    ]
    for copy in copies:
        copy.start()

    lab_pad[...] = jnp.zeros_like(lab_pad)
    lab_pad[:, :n_lab] = lab_ref[...]
    tab_rows = tab_v.shape[1]
    shape = (tab_rows, 128)
    cums, total = [], jnp.int32(0)
    lens, nus = [], []
    for b in range(n_utt):
        n_t = jnp.clip((flen_ref[b] - t0 + OCT - 1) // OCT, 0, n_oct)
        nu = llen_ref[b] + 1
        cums.append(total)
        nus.append(nu)
        total = total + n_t * nu
    item = lax.broadcasted_iota(jnp.int32, shape, 0) * 128 + lax.broadcasted_iota(jnp.int32, shape, 1)
    item = jnp.minimum(item, total - 1)
    utt = jnp.zeros(shape, jnp.int32)
    base = jnp.zeros(shape, jnp.int32)
    width = jnp.ones(shape, jnp.int32)
    for b in range(n_utt):
        hit = item >= cums[b]
        utt = jnp.where(hit, b, utt)
        base = jnp.where(hit, cums[b], base)
        width = jnp.where(hit, nus[b], width)
    rest = item - base
    octet = jnp.zeros(shape, jnp.int32)
    for k in range(1, n_oct):
        octet = octet + jnp.where(rest >= k * width, 1, 0)
    pos = jnp.clip(rest - octet * width, 0, n_pos - 1)
    word = jnp.zeros(shape, jnp.int32)
    for b in range(n_utt):
        row = jnp.broadcast_to(lab_pad[b:b + 1, :], shape)
        word = jnp.where(utt == b, jnp.take_along_axis(row, pos, axis=1, mode="promise_in_bounds"), word)
    tab_v[0] = (utt * t_local + octet * OCT) + (utt * n_pos + pos) * 65536
    tab_v[1] = word + (octet * n_rows + utt * GROUP + pos) * 65536
    tab_copy = pltpu.make_async_copy(tab_v, tab_s, tab_sem)
    tab_copy.start()

    copies[0].wait()
    for k in range(vocab // 128):
        cols = pl.ds(k * 128, 128)
        w_t[cols, :] = wout_v[:, cols].T
        bias_t[cols, :] = jnp.broadcast_to(bout_ref[k:k + 1, :], (128, 128)).T
    copies[1].wait()
    copies[2].wait()
    a_v[...] = jnp.dot(enc_v[...], wenc_v[...], preferred_element_type=jnp.float32).astype(jnp.bfloat16).astype(jnp.float32)
    copies[3].wait()
    copies[4].wait()
    c_v[...] = jnp.dot(pred_v[...], wpred_v[...], preferred_element_type=jnp.float32).astype(jnp.bfloat16).astype(jnp.float32)
    tab_copy.wait()

    lane16 = lax.broadcasted_iota(jnp.int32, (16, 128), 1)
    spread_idx = lax.broadcasted_iota(jnp.int32, (16, 128), 0) * OCT + lane16 % OCT
    is_blank = lane16 % 16 < OCT
    lane_item = lax.broadcasted_iota(jnp.int32, (1, 128), 1) // OCT

    def fields(which, k):
        both = tab_s[which, k // 128, k % 128]
        return both & 65535, both >> 16

    def make_hidden(tile):
        for q in range(ITEMS // 2):
            parts = []
            for k in (2 * q, 2 * q + 1):
                a_row, c_row = fields(0, tile * ITEMS + k)
                parts.append(a_v[pl.ds(pl.multiple_of(a_row, OCT), OCT), :] + c_v[pl.ds(c_row, 1), :])
            hid[16 * q:16 * q + 16, :] = jnp.tanh(jnp.concatenate(parts, axis=0)).astype(jnp.bfloat16)

    def finish(tile):
        labs = [fields(1, tile * ITEMS + k) for k in range(ITEMS)]
        lab_z = []
        for g in range(2):
            acc = jnp.zeros((1, 128), jnp.float32)
            for k in range(16):
                z_row = (z_a, z_b)[g][pl.ds(labs[16 * g + k][0], 1), :]
                acc = jnp.where(lane_item == k, z_row, acc)
            lab_z.append(acc)
        blank_z = jnp.concatenate([z_a[0:1, :], z_b[0:1, :]], axis=1)
        mx = jnp.max(mx_v[...], axis=0, keepdims=True)
        part = jnp.zeros((8, 256), jnp.float32)
        for k in range(vocab // 128):
            rows = slice(k * 128, k * 128 + 128)
            z = jnp.concatenate([z_a[rows, :], z_b[rows, :]], axis=1)
            part = part + jnp.sum(jnp.exp(z - mx).reshape(16, 8, 256), axis=0)
        lse = mx + jnp.log(jnp.sum(part, axis=0, keepdims=True))
        for g in range(2):
            lanes = slice(128 * g, 128 * g + 128)
            blank_lp = jnp.broadcast_to(blank_z[:, lanes] - lse[:, lanes], (16, 128))
            label_lp = jnp.broadcast_to(lab_z[g] - lse[:, lanes], (16, 128))
            wide = jnp.where(is_blank, jnp.take_along_axis(blank_lp, spread_idx, axis=1, mode="promise_in_bounds"),
                             jnp.take_along_axis(label_lp, spread_idx, axis=1, mode="promise_in_bounds"))
            for k in range(16):
                o_v[pl.ds(labs[16 * g + k][1], 1), :] = wide[k:k + 1, :]

    def matmul():
        z = lax.dot_general(w_t[...], hid[...], (((1,), (1,)), ((), ())), preferred_element_type=jnp.float32)
        bias = bias_t[...]
        z = z + jnp.concatenate([bias, bias], axis=1)
        z_a[...] = z[:, :128]
        z_b[...] = z[:, 128:]
        mx_v[...] = jnp.max(z.reshape(vocab // 8, 8, 256), axis=0)

    n_tiles = (total + ITEMS - 1) // ITEMS

    @pl.when(n_tiles > 0)
    def _():
        make_hidden(0)
        matmul()
        make_hidden(jnp.minimum(1, n_tiles - 1))

        def step(i, _):
            finish(i - 1)
            matmul()
            make_hidden(jnp.minimum(i + 1, n_tiles - 1))
            return 0

        lax.fori_loop(1, n_tiles, step, 0)
        finish(n_tiles - 1)

    lane_b = lax.broadcasted_iota(jnp.int32, (1, n_rows), 1) // GROUP
    lane_u = lax.broadcasted_iota(jnp.int32, (1, n_rows), 1) % GROUP
    flen = jnp.zeros((1, n_rows), jnp.int32)
    llen = jnp.zeros((1, n_rows), jnp.int32)
    for b in range(n_utt):
        flen = jnp.where(lane_b == b, flen_ref[b], flen)
        llen = jnp.where(lane_b == b, llen_ref[b], llen)
    lane128 = lax.broadcasted_iota(jnp.int32, (128, 128), 1)
    frame8 = lax.broadcasted_iota(jnp.int32, (OCT, 128), 0)
    for r in range(n_rows // 128):
        merged = o_v[128 * r:128 * r + 128, :]
        for k in range(1, n_oct):
            merged = jnp.where(lane128 >= 16 * k, o_v[k * n_rows + 128 * r:k * n_rows + 128 * r + 128, :], merged)
        turned = merged.T
        lanes = slice(128 * r, 128 * r + 128)
        for k in range(n_oct):
            live = (t0 + k * OCT + frame8 < flen[:, lanes]) & (lane_u[:, lanes] <= llen[:, lanes])
            live_lab = live & (lane_u[:, lanes] < llen[:, lanes])
            blank_out[k * OCT:k * OCT + OCT, lanes] = jnp.where(live, turned[16 * k:16 * k + 8, :], 0.0)
            label_out[k * OCT:k * OCT + OCT, lanes] = jnp.where(live_lab, turned[16 * k + 8:16 * k + 16, :], NEG_FILL)


def log_add(x, y):
    return jnp.maximum(x, y) + jnp.log(1.0 + jnp.exp(-jnp.abs(x - y)))


def lattice_kernel(n_seq, blank_ref, label_ref, llen_ref, loss_ref,
                   blank_s, label_s, m_loc, m_recv, v_out, v_recv, send_sem, recv_sem, out_sem, in_sem):
    t_local, n_rows = blank_ref.shape
    n_pos = m_loc.shape[1]
    me = lax.axis_index("seq")
    first_handler = n_seq - N_HANDLERS
    mine = me >= first_handler
    my_hand = jnp.maximum(me - first_handler, 0)

    barrier = pltpu.get_barrier_semaphore()
    for k in range(1, n_seq):
        other = lax.rem(me + k, n_seq)

        @pl.when(mine | (other >= first_handler))
        def _():
            pl.semaphore_signal(barrier, inc=1, device_id={"seq": other}, device_id_type=MESH)

    n_skew = blank_s.shape[0]
    lane_u = lax.broadcasted_iota(jnp.int32, (n_skew, n_rows), 1) % GROUP
    fills = ((blank_ref, blank_s, 0.0), (label_ref, label_s, NEG_FILL))
    for src, dst, fill in fills:
        rows = jnp.concatenate([src[...], jnp.full((n_skew - t_local, n_rows), fill, jnp.float32)], axis=0)
        for bit in (1, 2, 4, 8, 16):
            rows = jnp.where((lane_u & bit) != 0, pltpu.roll(rows, bit, 0), rows)
        dst[...] = rows

    shape = (n_pos, n_rows)
    start = jnp.where(lax.broadcasted_iota(jnp.int32, shape, 0) == lax.broadcasted_iota(jnp.int32, shape, 1) % GROUP,
                      0.0, NEG_FILL)

    def diagonal(d, carry):
        stay, move = carry
        alpha = log_add(stay, pltpu.roll(move, 1, 1))
        return alpha + blank_s[pl.ds(d, 1), :], alpha + label_s[pl.ds(d, 1), :]

    stay, _ = lax.fori_loop(0, t_local + n_pos - 1, diagonal, (start, jnp.full(shape, NEG_FILL, jnp.float32)))
    for h in range(N_HANDLERS):
        m_loc[h] = stay[:, 128 * h:128 * h + 128]

    pl.semaphore_wait(barrier, jnp.where(mine, n_seq - 1, N_HANDLERS))

    def send_matrix(h):
        return pltpu.make_async_remote_copy(
            src_ref=m_loc.at[h], dst_ref=m_recv.at[me], send_sem=send_sem.at[h], recv_sem=recv_sem.at[me],
            device_id={"seq": first_handler + h}, device_id_type=MESH)

    for h in range(N_HANDLERS):
        @pl.when(me != first_handler + h)
        def _():
            send_matrix(h).start()

        @pl.when(me == first_handler + h)
        def _():
            m_recv[me] = m_loc[h]

    def send_row(k):
        return pltpu.make_async_remote_copy(
            src_ref=v_out, dst_ref=v_recv.at[my_hand], send_sem=out_sem.at[k], recv_sem=in_sem.at[my_hand],
            device_id={"seq": lax.rem(me + k, n_seq)}, device_id_type=MESH)

    @pl.when(mine)
    def _():
        def arrived(src):
            @pl.when(src != me)
            def _():
                pltpu.make_async_remote_copy(
                    src_ref=m_loc.at[0], dst_ref=m_recv.at[src], send_sem=send_sem.at[0], recv_sem=recv_sem.at[src],
                    device_id={"seq": src}, device_id_type=MESH).wait_recv()

        sub = lax.broadcasted_iota(jnp.int32, (n_pos, 128), 0)
        lane = lax.broadcasted_iota(jnp.int32, (n_pos, 128), 1)
        turn_idx = lane // GROUP * GROUP + sub

        def join(src, row):
            arrived(src)
            col = jnp.take_along_axis(jnp.broadcast_to(row, (n_pos, 128)), turn_idx, axis=1, mode="promise_in_bounds")
            terms = col + m_recv[src]
            top = jnp.max(terms, axis=0, keepdims=True)
            return top + jnp.log(jnp.sum(jnp.exp(terms - top), axis=0, keepdims=True))

        arrived(jnp.int32(0))
        row = m_recv[0, 0:1, :]
        row = lax.fori_loop(1, n_seq, join, row)
        sub8 = lax.broadcasted_iota(jnp.int32, (8, 128), 0)
        lane8 = lax.broadcasted_iota(jnp.int32, (8, 128), 1)
        want = jnp.full((8, 128), -1, jnp.int32)
        for b in range(llen_ref.shape[0]):
            want = jnp.where((my_hand * (128 // GROUP) + sub8) == b, llen_ref[b], want)
        keep = (lane8 // GROUP == sub8) & (lane8 % GROUP == want)
        column = jnp.sum(jnp.where(keep, row, 0.0), axis=1, keepdims=True)
        here = (lane8 == my_hand * (128 // GROUP) + sub8) & (sub8 < 128 // GROUP)
        v_out[...] = jnp.broadcast_to(jnp.sum(jnp.where(here, column, 0.0), axis=0, keepdims=True), (8, 128))
        for k in range(1, n_seq):
            send_row(k).start()
        v_recv[my_hand] = v_out[...]

    total = jnp.zeros((1, 128), jnp.float32)
    for h in range(N_HANDLERS):
        @pl.when(me != first_handler + h)
        def _():
            pltpu.make_async_remote_copy(
                src_ref=v_out, dst_ref=v_recv.at[h], send_sem=out_sem.at[0], recv_sem=in_sem.at[h],
                device_id={"seq": first_handler + h}, device_id_type=MESH).wait_recv()
    for h in range(N_HANDLERS):
        total = total + v_recv[h, 0:1, :]
    loss_ref[...] = -total[:, :loss_ref.shape[1]]

    for h in range(N_HANDLERS):
        @pl.when(me != first_handler + h)
        def _():
            send_matrix(h).wait_send()

    @pl.when(mine)
    def _():
        for k in range(1, n_seq):
            send_row(k).wait_send()


def solution(mesh):
    n_seq = mesh.shape["seq"]

    def local_loss(enc_blk, pred_out, w_enc, w_pred, w_out, b_out, labels, frame_len, label_len):
        n_utt, t_local, d_enc = enc_blk.shape
        n_pos, d_pred = pred_out.shape[1:]
        joint, vocab = w_out.shape
        n_rows = n_utt * GROUP
        n_oct = t_local // OCT
        max_items = n_utt * n_pos * n_oct
        tab_rows = -(-(max_items + ITEMS) // 1024) * 8
        hbm = pl.BlockSpec(memory_space=pl.ANY)
        vmem = pl.BlockSpec(memory_space=pltpu.VMEM)
        smem = pl.BlockSpec(memory_space=pltpu.SMEM)
        f32, bf16 = jnp.float32, jnp.bfloat16
        lattice_shape = jax.ShapeDtypeStruct((t_local, n_rows), f32)
        blank, label = pl.pallas_call(
            joint_kernel,
            out_shape=(lattice_shape, lattice_shape),
            in_specs=[hbm] * 5 + [vmem, vmem, smem, smem],
            out_specs=(vmem, vmem),
            scratch_shapes=[
                pltpu.VMEM((n_utt * t_local, d_enc), bf16),
                pltpu.VMEM((n_utt * n_pos, d_pred), bf16),
                pltpu.VMEM((d_enc, joint), bf16),
                pltpu.VMEM((d_pred, joint), bf16),
                pltpu.VMEM((joint, vocab), bf16),
                pltpu.VMEM((vocab, joint), bf16),
                pltpu.VMEM((vocab, 128), f32),
                pltpu.VMEM((n_utt * t_local, joint), f32),
                pltpu.VMEM((n_utt * n_pos, joint), f32),
                pltpu.VMEM((ITEMS * OCT, joint), bf16),
                pltpu.VMEM((vocab, 128), f32),
                pltpu.VMEM((vocab, 128), f32),
                pltpu.VMEM((8, ITEMS * OCT), f32),
                pltpu.VMEM((n_oct * n_rows, 128), f32),
                pltpu.VMEM((n_utt, 128), jnp.int32),
                pltpu.VMEM((2, tab_rows, 128), jnp.int32),
                pltpu.SMEM((2, tab_rows, 128), jnp.int32),
                pltpu.SemaphoreType.DMA((5,)),
                pltpu.SemaphoreType.DMA,
            ],
            name="joint",
        )(enc_blk.reshape(n_utt * t_local, d_enc), pred_out.reshape(n_utt * n_pos, d_pred), w_enc, w_pred, w_out,
          b_out.reshape(vocab // 128, 128), labels, frame_len, label_len)

        loss = pl.pallas_call(
            functools.partial(lattice_kernel, n_seq),
            out_shape=jax.ShapeDtypeStruct((1, n_utt), f32),
            in_specs=[vmem, vmem, smem],
            out_specs=vmem,
            scratch_shapes=[
                pltpu.VMEM((t_local + n_pos, n_rows), f32),
                pltpu.VMEM((t_local + n_pos, n_rows), f32),
                pltpu.VMEM((N_HANDLERS, n_pos, 128), f32),
                pltpu.VMEM((n_seq, n_pos, 128), f32),
                pltpu.VMEM((8, 128), f32),
                pltpu.VMEM((N_HANDLERS, 8, 128), f32),
                pltpu.SemaphoreType.DMA((N_HANDLERS,)),
                pltpu.SemaphoreType.DMA((n_seq,)),
                pltpu.SemaphoreType.DMA((n_seq,)),
                pltpu.SemaphoreType.DMA((N_HANDLERS,)),
            ],
            compiler_params=pltpu.CompilerParams(collective_id=0, has_side_effects=True),
            name="lattice",
        )(blank, label, label_len)
        return loss.reshape(n_utt)

    in_specs = (P("dp", "seq", None), P("dp", None, None), P(), P(), P(), P(), P("dp", None), P("dp"), P("dp"))
    return jax.shard_map(local_loss, mesh=mesh, in_specs=in_specs, out_specs=P("dp"), check_vma=False)
```

time: 469 us -> 44.6 us (0.10); the launches traced: 463 us -> 44.3 us
  other arithmetic: 314 us -> 0 us
  starting transfers between devices: 67.6 us -> 0 us
  Pallas kernels: 0 us -> 43.2 us
  blocking collectives: 34.1 us -> 0 us
  matrix products: 18.3 us -> 0 us
  local copies, waits for them, and re-layouts: 14.8 us -> 1.1 us
  waiting for transfers between devices: 12.3 us -> 0 us
    another operation x385 -> x0, other arithmetic: 249 us -> none  [the longest x384 238 us: frame_step(): lax.cumlogsumexp(row_prev - cum_label, axis=1)]
    ppermute x15 -> x0, starting transfers between devices: 67.6 us -> none  [relay_hop(): passed = lax.ppermute(last_row, 'seq', shift_perm)]
    pallas_call x0 -> x2, Pallas kernels: none -> 43.2 us  [the longest x1 22.7 us: local_loss(): pl.pallas_call(joint_kernel, out_shape=(lattice_shape, lattice_shape), in...]
    psum x1 -> x0, blocking collectives: 34.1 us -> none  [local_loss(): return -lax.psum(picked, 'seq')]
    dot_general x26 -> x0, matrix products: 18.3 us -> none  [the longest x24 16.2 us: frame_logprobs(): jnp.einsum('kbpj,jv->kbpv', hidden, w_out, preferred_element_type=jnp.flo...]
    convert_element_type x24 -> x0, other arithmetic: 17.3 us -> none  [frame_logprobs(): enc_rows.astype(jnp.float32)[:, :, None, :] + pred_f32[None]]
    while x48 -> x0, other arithmetic: 15.6 us -> none
    dynamic_update_slice x72 -> x0, other arithmetic: 15.5 us -> none  [the longest x48 15.4 us: local_loss(): blank_all, label_all = lax.map(step_fn, enc_proj[:, None])]
  transfers between devices with their start and end apart: 15 -> 0, of which waited for: 15 -> 0; matrix products, arithmetic and copies ran while one was open for 0% -> 0% of each run, Pallas kernels for 0% -> 0%
where the time goes in v1:
time: 44.6 us; the launch traced here: 44.3 us
  Pallas kernels  43.2 us (97%)
  local copies, waits for them, and re-layouts  1.1 us (2%)
    pallas_call x1, Pallas kernels, local_loss(): pl.pallas_call(joint_kernel, out_shape=(lattice_shape, lattice_shape), in...  22.7 us
    pallas_call x1, Pallas kernels, local_loss(): pl.pallas_call(functools.partial(lattice_kernel, n_seq), out_shape=jax.Sh...  20.5 us
    unnamed x3, local copies, waits for them, and re-layouts  1.1 us

profile of v1, /device:TPU:21, one launch (start us, length us, event | category | flops | bytes accessed | tf_op | source)
XLA Modules:
  0.0 44.3 jit_solution(2111462744845973884)
XLA Ops:
  0.0 22.7 %joint.1 = (f32[24,512]{1,0:T(8,128)}, f32[24,512]{1,0:T(8,128)}) custom-call(bf16[384,1024]{1,0:T(8,128)(2,1)} %bitcast.4, bf16[384,320]{1,0:T(8,128)(2,1)} %bitcast.5, bf16[1024,512]{1,0:T(8,128)(2,1)} %wenc_hbm.1, bf16[320,512]{1,0:T(8,128)(2,1)} %wpred_hbm.1, bf16[512,1024]{1,0:T(8,128)(2,1)} %wout_hbm.1, f32[8,128]{1,0:T(8,128)} %bitcast.6, ...), custom_call_target="tpu_custom_call" | custom-call | tf_op jit(solution)/shard_map/joint/pallas_call | solution.py:314
  22.7 20.5 %lattice.1 = f32[1,16]{1,0:T(1,128)} custom-call(f32[24,512]{1,0:T(8,128)} %get-tuple-element.7.blank_ref, f32[24,512]{1,0:T(8,128)} %get-tuple-element.8.label_ref, s32[16]{0:T(128)} %llen_ref.3), custom_call_target="tpu_custom_call" | custom-call | tf_op jit(solution)/shard_map/lattice/pallas_call | solution.py:344
  43.2 0.0 copy-start
  43.2 0.6 %copy-done = f32[1,16]{1,0:T(1,128)S(1)} copy-done((f32[1,16]{1,0:T(1,128)S(1)}, f32[1,16]{1,0:T(1,128)}, u32[]{:S(2)}) %copy-start) | copy-done | bytes 88
  43.8 0.5 %copy.11 = f32[16]{0:T(128)} copy(f32[16]{0:T(128)S(1)} %bitcast.7) | data formatting | bytes 128
Async XLA Ops:
  43.2 0.6 %copy-start = (f32[1,16]{1,0:T(1,128)S(1)}, f32[1,16]{1,0:T(1,128)}, u32[]{:S(2)}) copy-start(f32[1,16]{1,0:T(1,128)} %lattice.1) | copy-start | bytes 196
